TPU v7x, 256 devices: a whole 4x4x8 slice. The times are simulated.
256 devices in a mesh: pipe: 8 (over x, z_lo), tensor: 4 (over y), expert: 8 (over z_hi, core).
Axes of the slice: x: 4, y: 4, z: 8 (z_hi: 4, z_lo: 2; z = z_hi * 2 + z_lo), core: 2. Of those that a mesh axis runs over, the one named last changes fastest.
Arguments:
- tokens: bfloat16 [2, 512, 4096], P(None, 'expert'), may hold values from -6 to 6
- gains: float32 [8, 4096], P('pipe'), may hold values from 0.1 to 1.9
- route_ids: int32 [8, 2, 512, 2], P('pipe', None, 'expert'), may hold values from 0 to 7, all different within a row
- route_weights: float32 [8, 2, 512, 2], P('pipe', None, 'expert'), may hold values from 0.2 to 1
- picks: int32 [8, 2, 8, 64], P('pipe', None, 'expert'), may hold values from 0 to 63, each once within a row
- w_gate: bfloat16 [8, 8, 4096, 1536], P('pipe', 'expert', None, 'tensor'), may hold values from -0.09375 to 0.09375
- w_up: bfloat16 [8, 8, 4096, 1536], P('pipe', 'expert', None, 'tensor'), may hold values from -0.09375 to 0.09375
- w_down: bfloat16 [8, 8, 1536, 4096], P('pipe', 'expert', 'tensor'), may hold values from -0.15625 to 0.15625
Outputs:
- streams: bfloat16 [8, 2, 512, 4096], P('pipe', None, 'expert', 'tensor')
Inputs may be any that keep to these rules, and one draw needn't show every extreme that they name: `route_ids`: each token names 2 different experts; every expert is named by some token. `picks`: for every layer, micro-batch and block of 64 tokens, a permutation of 0 to 63.
All inputs are finite; a program needn't handle non-finite values.
Results may differ from a plain program's by a relative error of at most 0.025.
Values may be sent and summed in bfloat16 or wider, within the bound.
A program may use at most 64 MiB of HBM per device.

v0:
```python
import jax
import jax.numpy as jnp
from jax import lax
from jax.sharding import PartitionSpec as P

epsilon = 1e-06


def from_everyone(value, axis):
    copies = jnp.broadcast_to(value, (lax.axis_size(axis), *value.shape))
    return lax.all_to_all(copies, axis, split_axis=0, concat_axis=0, tiled=True)


def joined_along(pieces, dim):
    pieces = jnp.moveaxis(pieces, 0, dim)
    shape = pieces.shape
    return pieces.reshape(*shape[:dim], shape[dim] * shape[dim + 1], *shape[dim + 2 :])


def gather_directly(value, axis, dim):
    pieces = from_everyone(value, axis)
    return joined_along(pieces, dim)


def cut_along(value, dim, count):
    before, after = (value.shape[:dim], value.shape[dim + 1 :])
    return jnp.moveaxis(value.reshape(*before, count, -1, *after), dim, 0)


def sum_at_owner(value, axis, dim):
    pieces = cut_along(value, dim, lax.axis_size(axis))
    arrived = lax.all_to_all(pieces, axis, split_axis=0, concat_axis=0, tiled=True)
    return arrived.astype(jnp.float32).sum(axis=0)


def passed_along(block, axis, distance):
    devices = range(lax.axis_size(axis))
    route = [(i - distance, i) for i in devices if i - distance in devices]
    return lax.ppermute(block, axis, route)


def local(tokens, gains, route_ids, route_weights, picks, w_gate, w_up, w_down):
    micro_count = tokens.shape[0]
    local_tokens = tokens.shape[1]
    model_width = tokens.shape[2]
    route_count = route_ids.shape[3]
    tensor_ranks = lax.axis_size("tensor")
    groups = lax.axis_size("expert")
    sections = lax.axis_size("pipe")
    quarter = local_tokens // tensor_ranks
    capacity = 4 * quarter * route_count // (3 * groups)
    slice_width = model_width // tensor_ranks
    my_section = lax.axis_index("pipe")
    my_rank = lax.axis_index("tensor")
    gain_row = gains[0]
    gate_matrix = w_gate[0, 0]
    up_matrix = w_up[0, 0]
    down_matrix = w_down[0, 0]

    def expert_work(arrived):
        gathered = gather_directly(arrived, "tensor", 0)
        row_count = gathered.shape[0] * gathered.shape[1]
        row_block = gathered.reshape(row_count, model_width)
        gate_val = jnp.dot(row_block, gate_matrix, preferred_element_type=jnp.float32)
        up_val = jnp.dot(row_block, up_matrix, preferred_element_type=jnp.float32)
        hidden = (jax.nn.silu(gate_val) * up_val).astype(jnp.bfloat16)
        partial_sum = jnp.dot(hidden, down_matrix, preferred_element_type=jnp.float32)
        summed = sum_at_owner(partial_sum.reshape(gathered.shape).astype(jnp.bfloat16), "tensor", 0)
        return summed.astype(jnp.bfloat16)

    def expert_layer(quarter_rows, chosen, micro_index):
        section_ids = route_ids[0, micro_index][chosen]
        section_weights = route_weights[0, micro_index][chosen]
        stream_f = quarter_rows.astype(jnp.float32)
        inv_rms = lax.rsqrt(jnp.mean(stream_f * stream_f, axis=1, keepdims=True) + epsilon)
        normed = (stream_f * inv_rms * gain_row[None, :]).astype(jnp.bfloat16)
        flat_ids = section_ids.reshape(-1)
        onehot = (flat_ids[:, None] == jnp.arange(groups, dtype=jnp.int32)[None, :]).astype(
            jnp.int32
        )
        earlier = jnp.cumsum(onehot, axis=0) - onehot
        slot_index = jnp.sum(earlier * onehot, axis=1)
        kept_mask = slot_index < capacity
        target = jnp.where(kept_mask, flat_ids * capacity + slot_index, groups * capacity)
        placing = (
            jnp.arange(groups * capacity, dtype=jnp.int32)[:, None] == target[None, :]
        ).astype(jnp.bfloat16)
        routed = jnp.repeat(normed, route_count, axis=0)
        outgoing = jnp.dot(placing, routed, preferred_element_type=jnp.float32).astype(jnp.bfloat16)
        outgoing = outgoing.reshape(groups, capacity, model_width)
        returned = expert_work(
            lax.all_to_all(outgoing, "expert", split_axis=0, concat_axis=0, tiled=True)
        )
        homeward = lax.all_to_all(returned, "expert", split_axis=0, concat_axis=0, tiled=True)
        flat_back = jnp.concatenate(
            [
                homeward.reshape(groups * capacity, model_width),
                jnp.zeros((1, model_width), jnp.bfloat16),
            ],
            axis=0,
        )
        picked = flat_back[target].astype(jnp.float32).reshape(quarter, route_count, model_width)
        kept_grid = kept_mask.reshape(quarter, route_count)
        weighted = picked * (section_weights * kept_grid)[..., None]
        update = jnp.sum(weighted, axis=1)
        return (stream_f + update).astype(jnp.bfloat16)

    def run_section(stream, micro_index):
        order_all = picks[0, micro_index, 0]
        chosen = lax.dynamic_slice_in_dim(order_all, my_rank * quarter, quarter)
        permuted = stream[order_all]
        quarter_rows = lax.all_to_all(permuted, "tensor", split_axis=0, concat_axis=1, tiled=True)
        fresh_rows = expert_layer(quarter_rows, chosen, micro_index)
        spread = lax.all_to_all(fresh_rows, "tensor", split_axis=1, concat_axis=0, tiled=True)
        return jnp.zeros_like(stream).at[order_all].set(spread)

    def first_input(micro_index):
        whole = tokens[micro_index]
        return lax.dynamic_slice_in_dim(whole, my_rank * slice_width, slice_width, 1)

    def send_on(fresh):
        return passed_along(fresh, "pipe", 1)

    def section_tick(carry, tick_index):
        arrived, collected = carry
        micro_index = tick_index - my_section
        active = (micro_index >= 0) & (micro_index < micro_count)
        clipped = jnp.clip(micro_index, 0, micro_count - 1)
        stream = jnp.where(my_section == 0, first_input(clipped), arrived)
        computed = run_section(stream, clipped)
        fresh = jnp.where(active, computed, stream)
        written = collected.at[clipped].set(fresh)
        collected = jnp.where(active, written, collected)
        return ((send_on(fresh), collected), None)

    empty_state = jnp.zeros((local_tokens, slice_width), jnp.bfloat16)
    collected = jnp.zeros((micro_count, local_tokens, slice_width), jnp.bfloat16)
    ticks = jnp.arange(micro_count + sections - 1, dtype=jnp.int32)
    (final_state, collected), unused = lax.scan(section_tick, (empty_state, collected), ticks)
    return collected[None]


def solution(mesh):
    return jax.shard_map(
        local,
        mesh=mesh,
        in_specs=(
            P(None, "expert", None),
            P("pipe", None),
            P("pipe", None, "expert", None),
            P("pipe", None, "expert", None),
            P("pipe", None, "expert", None),
            P("pipe", "expert", None, "tensor"),
            P("pipe", "expert", None, "tensor"),
            P("pipe", "expert", "tensor", None),
        ),
        out_specs=P("pipe", None, "expert", "tensor"),
        check_vma=False,
    )
```

profile of v0, /device:TPU:32, one launch (start us, length us, event | category | flops | bytes accessed | tf_op | source)
XLA Modules:
  0.0 1171.1 jit_solution(10860606724604831986)
XLA Ops:
  1.3 1169.9 %while.16 = (s32[]{:T(128)}, bf16[64,1024]{1,0:T(8,128)(2,1)S(1)}, bf16[2,64,1024]{2,1,0:T(8,128)(2,1)}, s32[9]{0:T(128)}, s32[]{:T(128)}, /*index=5*/s32[1,2,1,...) while((s32[]{:T(128)}, bf16[64,1024]{1,0:T(8,128)(2,1)S(1)}, ...), condition=%wide.region_8.9_spmd, body=%wide.region_0.8_spmd.sunk | while | flops 1523243264 | bytes 51076840 | solution.py:139
  17.6 23.8 %all_to_all.92 = bf16[8,5,4096]{2,1,0:T(8,128)(2,1)S(1)} all-to-all(bf16[8,5,4096]{2,1,0:T(8,128)(2,1)S(1)} %reshape.340), channel_id=1, replica_groups=mesh['pipe'=8,'tensor'=4,'expert'=8] {'expert'}, dimensions={0} | all-to-all | bytes 655360 | tf_op jit(solution)/shard_map/while/body/eval_jaxpr/all_to_all | solution.py:92
  41.7 20.4 %all_to_all.93 = bf16[4,8,5,4096]{3,1,2,0:T(8,128)(2,1)S(1)} all-to-all(bf16[4,8,5,4096]{3,1,2,0:T(8,128)(2,1)S(1)} %broadcast_in_dim.48), channel_id=1, replica_groups=mesh['pipe'=8,'tensor'=4,'expert'=8] {'tensor'}, dimensions={0} | all-to-all | bytes 2621440 | tf_op jit(solution)/shard_map/while/body/eval_jaxpr/all_to_all | solution.py:11
  77.0 16.9 %all-to-all-done.3 = bf16[4,8,5,4096]{3,1,2,0:T(8,128)(2,1)S(1)} async-done(((bf16[4,8,5,4096]{3,1,2,0:T(8,128)(2,1)}), bf16[4,8,5,4096]{3,1,2,0:T(8,128)(2,1)S(1)}, u32[]{:S(2)}, u32[]{:S(2)}) %all-to-all-start.3) | async-done | bytes 1310752 | tf_op jit(solution)/shard_map/while/body/eval_jaxpr/all_to_all | solution.py:32
  99.6 17.0 %all-to-all-done.4 = bf16[8,5,4096]{2,1,0:T(8,128)(2,1)S(1)} async-done(((bf16[8,5,4096]{2,1,0:T(8,128)(2,1)}), bf16[8,5,4096]{2,1,0:T(8,128)(2,1)S(1)}, u32[]{:S(2)}, u32[]{:S(2)}) %all-to-all-start.4) | async-done | bytes 327712 | tf_op jit(solution)/shard_map/while/body/eval_jaxpr/all_to_all | solution.py:94
  123.4 5.2 all-to-all-done.5
  152.3 19.0 %all_to_all.92 = bf16[8,5,4096]{2,1,0:T(8,128)(2,1)S(1)} all-to-all(bf16[8,5,4096]{2,1,0:T(8,128)(2,1)S(1)} %reshape.340), channel_id=1, replica_groups=mesh['pipe'=8,'tensor'=4,'expert'=8] {'expert'}, dimensions={0} | all-to-all | bytes 655360 | tf_op jit(solution)/shard_map/while/body/eval_jaxpr/all_to_all | solution.py:92
  171.6 20.7 %all_to_all.93 = bf16[4,8,5,4096]{3,1,2,0:T(8,128)(2,1)S(1)} all-to-all(bf16[4,8,5,4096]{3,1,2,0:T(8,128)(2,1)S(1)} %broadcast_in_dim.48), channel_id=1, replica_groups=mesh['pipe'=8,'tensor'=4,'expert'=8] {'tensor'}, dimensions={0} | all-to-all | bytes 2621440 | tf_op jit(solution)/shard_map/while/body/eval_jaxpr/all_to_all | solution.py:11
  207.1 17.0 %all-to-all-done.3 = bf16[4,8,5,4096]{3,1,2,0:T(8,128)(2,1)S(1)} async-done(((bf16[4,8,5,4096]{3,1,2,0:T(8,128)(2,1)}), bf16[4,8,5,4096]{3,1,2,0:T(8,128)(2,1)S(1)}, u32[]{:S(2)}, u32[]{:S(2)}) %all-to-all-start.3) | async-done | bytes 1310752 | tf_op jit(solution)/shard_map/while/body/eval_jaxpr/all_to_all | solution.py:32
  229.8 14.3 %all-to-all-done.4 = bf16[8,5,4096]{2,1,0:T(8,128)(2,1)S(1)} async-done(((bf16[8,5,4096]{2,1,0:T(8,128)(2,1)}), bf16[8,5,4096]{2,1,0:T(8,128)(2,1)S(1)}, u32[]{:S(2)}, u32[]{:S(2)}) %all-to-all-start.4) | async-done | bytes 327712 | tf_op jit(solution)/shard_map/while/body/eval_jaxpr/all_to_all | solution.py:94
  250.9 5.2 all-to-all-done.5
  257.8 5.0 collective-permute-start
  280.4 19.1 %all_to_all.92 = bf16[8,5,4096]{2,1,0:T(8,128)(2,1)S(1)} all-to-all(bf16[8,5,4096]{2,1,0:T(8,128)(2,1)S(1)} %reshape.340), channel_id=1, replica_groups=mesh['pipe'=8,'tensor'=4,'expert'=8] {'expert'}, dimensions={0} | all-to-all | bytes 655360 | tf_op jit(solution)/shard_map/while/body/eval_jaxpr/all_to_all | solution.py:92
  299.9 20.7 %all_to_all.93 = bf16[4,8,5,4096]{3,1,2,0:T(8,128)(2,1)S(1)} all-to-all(bf16[4,8,5,4096]{3,1,2,0:T(8,128)(2,1)S(1)} %broadcast_in_dim.48), channel_id=1, replica_groups=mesh['pipe'=8,'tensor'=4,'expert'=8] {'tensor'}, dimensions={0} | all-to-all | bytes 2621440 | tf_op jit(solution)/shard_map/while/body/eval_jaxpr/all_to_all | solution.py:11
  335.4 17.0 %all-to-all-done.3 = bf16[4,8,5,4096]{3,1,2,0:T(8,128)(2,1)S(1)} async-done(((bf16[4,8,5,4096]{3,1,2,0:T(8,128)(2,1)}), bf16[4,8,5,4096]{3,1,2,0:T(8,128)(2,1)S(1)}, u32[]{:S(2)}, u32[]{:S(2)}) %all-to-all-start.3) | async-done | bytes 1310752 | tf_op jit(solution)/shard_map/while/body/eval_jaxpr/all_to_all | solution.py:32
  358.1 14.1 %all-to-all-done.4 = bf16[8,5,4096]{2,1,0:T(8,128)(2,1)S(1)} async-done(((bf16[8,5,4096]{2,1,0:T(8,128)(2,1)}), bf16[8,5,4096]{2,1,0:T(8,128)(2,1)S(1)}, u32[]{:S(2)}, u32[]{:S(2)}) %all-to-all-start.4) | async-done | bytes 327712 | tf_op jit(solution)/shard_map/while/body/eval_jaxpr/all_to_all | solution.py:94
  379.1 5.2 all-to-all-done.5
  385.9 5.3 collective-permute-start
  408.8 20.4 %all_to_all.92 = bf16[8,5,4096]{2,1,0:T(8,128)(2,1)S(1)} all-to-all(bf16[8,5,4096]{2,1,0:T(8,128)(2,1)S(1)} %reshape.340), channel_id=1, replica_groups=mesh['pipe'=8,'tensor'=4,'expert'=8] {'expert'}, dimensions={0} | all-to-all | bytes 655360 | tf_op jit(solution)/shard_map/while/body/eval_jaxpr/all_to_all | solution.py:92
  429.6 20.7 %all_to_all.93 = bf16[4,8,5,4096]{3,1,2,0:T(8,128)(2,1)S(1)} all-to-all(bf16[4,8,5,4096]{3,1,2,0:T(8,128)(2,1)S(1)} %broadcast_in_dim.48), channel_id=1, replica_groups=mesh['pipe'=8,'tensor'=4,'expert'=8] {'tensor'}, dimensions={0} | all-to-all | bytes 2621440 | tf_op jit(solution)/shard_map/while/body/eval_jaxpr/all_to_all | solution.py:11
  465.1 17.0 %all-to-all-done.3 = bf16[4,8,5,4096]{3,1,2,0:T(8,128)(2,1)S(1)} async-done(((bf16[4,8,5,4096]{3,1,2,0:T(8,128)(2,1)}), bf16[4,8,5,4096]{3,1,2,0:T(8,128)(2,1)S(1)}, u32[]{:S(2)}, u32[]{:S(2)}) %all-to-all-start.3) | async-done | bytes 1310752 | tf_op jit(solution)/shard_map/while/body/eval_jaxpr/all_to_all | solution.py:32
  487.8 14.2 %all-to-all-done.4 = bf16[8,5,4096]{2,1,0:T(8,128)(2,1)S(1)} async-done(((bf16[8,5,4096]{2,1,0:T(8,128)(2,1)}), bf16[8,5,4096]{2,1,0:T(8,128)(2,1)S(1)}, u32[]{:S(2)}, u32[]{:S(2)}) %all-to-all-start.4) | async-done | bytes 327712 | tf_op jit(solution)/shard_map/while/body/eval_jaxpr/all_to_all | solution.py:94
  508.8 5.2 all-to-all-done.5
  537.6 21.3 %all_to_all.92 = bf16[8,5,4096]{2,1,0:T(8,128)(2,1)S(1)} all-to-all(bf16[8,5,4096]{2,1,0:T(8,128)(2,1)S(1)} %reshape.340), channel_id=1, replica_groups=mesh['pipe'=8,'tensor'=4,'expert'=8] {'expert'}, dimensions={0} | all-to-all | bytes 655360 | tf_op jit(solution)/shard_map/while/body/eval_jaxpr/all_to_all | solution.py:92
  559.3 20.7 %all_to_all.93 = bf16[4,8,5,4096]{3,1,2,0:T(8,128)(2,1)S(1)} all-to-all(bf16[4,8,5,4096]{3,1,2,0:T(8,128)(2,1)S(1)} %broadcast_in_dim.48), channel_id=1, replica_groups=mesh['pipe'=8,'tensor'=4,'expert'=8] {'tensor'}, dimensions={0} | all-to-all | bytes 2621440 | tf_op jit(solution)/shard_map/while/body/eval_jaxpr/all_to_all | solution.py:11
  594.9 17.0 %all-to-all-done.3 = bf16[4,8,5,4096]{3,1,2,0:T(8,128)(2,1)S(1)} async-done(((bf16[4,8,5,4096]{3,1,2,0:T(8,128)(2,1)}), bf16[4,8,5,4096]{3,1,2,0:T(8,128)(2,1)S(1)}, u32[]{:S(2)}, u32[]{:S(2)}) %all-to-all-start.3) | async-done | bytes 1310752 | tf_op jit(solution)/shard_map/while/body/eval_jaxpr/all_to_all | solution.py:32
  617.6 14.2 %all-to-all-done.4 = bf16[8,5,4096]{2,1,0:T(8,128)(2,1)S(1)} async-done(((bf16[8,5,4096]{2,1,0:T(8,128)(2,1)}), bf16[8,5,4096]{2,1,0:T(8,128)(2,1)S(1)}, u32[]{:S(2)}, u32[]{:S(2)}) %all-to-all-start.4) | async-done | bytes 327712 | tf_op jit(solution)/shard_map/while/body/eval_jaxpr/all_to_all | solution.py:94
  638.5 5.2 all-to-all-done.5
  667.4 21.3 %all_to_all.92 = bf16[8,5,4096]{2,1,0:T(8,128)(2,1)S(1)} all-to-all(bf16[8,5,4096]{2,1,0:T(8,128)(2,1)S(1)} %reshape.340), channel_id=1, replica_groups=mesh['pipe'=8,'tensor'=4,'expert'=8] {'expert'}, dimensions={0} | all-to-all | bytes 655360 | tf_op jit(solution)/shard_map/while/body/eval_jaxpr/all_to_all | solution.py:92
  689.1 20.7 %all_to_all.93 = bf16[4,8,5,4096]{3,1,2,0:T(8,128)(2,1)S(1)} all-to-all(bf16[4,8,5,4096]{3,1,2,0:T(8,128)(2,1)S(1)} %broadcast_in_dim.48), channel_id=1, replica_groups=mesh['pipe'=8,'tensor'=4,'expert'=8] {'tensor'}, dimensions={0} | all-to-all | bytes 2621440 | tf_op jit(solution)/shard_map/while/body/eval_jaxpr/all_to_all | solution.py:11
  724.6 17.0 %all-to-all-done.3 = bf16[4,8,5,4096]{3,1,2,0:T(8,128)(2,1)S(1)} async-done(((bf16[4,8,5,4096]{3,1,2,0:T(8,128)(2,1)}), bf16[4,8,5,4096]{3,1,2,0:T(8,128)(2,1)S(1)}, u32[]{:S(2)}, u32[]{:S(2)}) %all-to-all-start.3) | async-done | bytes 1310752 | tf_op jit(solution)/shard_map/while/body/eval_jaxpr/all_to_all | solution.py:32
  747.3 14.2 %all-to-all-done.4 = bf16[8,5,4096]{2,1,0:T(8,128)(2,1)S(1)} async-done(((bf16[8,5,4096]{2,1,0:T(8,128)(2,1)}), bf16[8,5,4096]{2,1,0:T(8,128)(2,1)S(1)}, u32[]{:S(2)}, u32[]{:S(2)}) %all-to-all-start.4) | async-done | bytes 327712 | tf_op jit(solution)/shard_map/while/body/eval_jaxpr/all_to_all | solution.py:94
  768.2 5.2 all-to-all-done.5
  797.1 21.3 %all_to_all.92 = bf16[8,5,4096]{2,1,0:T(8,128)(2,1)S(1)} all-to-all(bf16[8,5,4096]{2,1,0:T(8,128)(2,1)S(1)} %reshape.340), channel_id=1, replica_groups=mesh['pipe'=8,'tensor'=4,'expert'=8] {'expert'}, dimensions={0} | all-to-all | bytes 655360 | tf_op jit(solution)/shard_map/while/body/eval_jaxpr/all_to_all | solution.py:92
  818.8 20.7 %all_to_all.93 = bf16[4,8,5,4096]{3,1,2,0:T(8,128)(2,1)S(1)} all-to-all(bf16[4,8,5,4096]{3,1,2,0:T(8,128)(2,1)S(1)} %broadcast_in_dim.48), channel_id=1, replica_groups=mesh['pipe'=8,'tensor'=4,'expert'=8] {'tensor'}, dimensions={0} | all-to-all | bytes 2621440 | tf_op jit(solution)/shard_map/while/body/eval_jaxpr/all_to_all | solution.py:11
  854.3 17.0 %all-to-all-done.3 = bf16[4,8,5,4096]{3,1,2,0:T(8,128)(2,1)S(1)} async-done(((bf16[4,8,5,4096]{3,1,2,0:T(8,128)(2,1)}), bf16[4,8,5,4096]{3,1,2,0:T(8,128)(2,1)S(1)}, u32[]{:S(2)}, u32[]{:S(2)}) %all-to-all-start.3) | async-done | bytes 1310752 | tf_op jit(solution)/shard_map/while/body/eval_jaxpr/all_to_all | solution.py:32
  877.0 14.2 %all-to-all-done.4 = bf16[8,5,4096]{2,1,0:T(8,128)(2,1)S(1)} async-done(((bf16[8,5,4096]{2,1,0:T(8,128)(2,1)}), bf16[8,5,4096]{2,1,0:T(8,128)(2,1)S(1)}, u32[]{:S(2)}, u32[]{:S(2)}) %all-to-all-start.4) | async-done | bytes 327712 | tf_op jit(solution)/shard_map/while/body/eval_jaxpr/all_to_all | solution.py:94
  898.0 5.2 all-to-all-done.5
  926.8 21.3 %all_to_all.92 = bf16[8,5,4096]{2,1,0:T(8,128)(2,1)S(1)} all-to-all(bf16[8,5,4096]{2,1,0:T(8,128)(2,1)S(1)} %reshape.340), channel_id=1, replica_groups=mesh['pipe'=8,'tensor'=4,'expert'=8] {'expert'}, dimensions={0} | all-to-all | bytes 655360 | tf_op jit(solution)/shard_map/while/body/eval_jaxpr/all_to_all | solution.py:92
  948.5 20.7 %all_to_all.93 = bf16[4,8,5,4096]{3,1,2,0:T(8,128)(2,1)S(1)} all-to-all(bf16[4,8,5,4096]{3,1,2,0:T(8,128)(2,1)S(1)} %broadcast_in_dim.48), channel_id=1, replica_groups=mesh['pipe'=8,'tensor'=4,'expert'=8] {'tensor'}, dimensions={0} | all-to-all | bytes 2621440 | tf_op jit(solution)/shard_map/while/body/eval_jaxpr/all_to_all | solution.py:11
  984.0 17.0 %all-to-all-done.3 = bf16[4,8,5,4096]{3,1,2,0:T(8,128)(2,1)S(1)} async-done(((bf16[4,8,5,4096]{3,1,2,0:T(8,128)(2,1)}), bf16[4,8,5,4096]{3,1,2,0:T(8,128)(2,1)S(1)}, u32[]{:S(2)}, u32[]{:S(2)}) %all-to-all-start.3) | async-done | bytes 1310752 | tf_op jit(solution)/shard_map/while/body/eval_jaxpr/all_to_all | solution.py:32
  1006.7 14.2 %all-to-all-done.4 = bf16[8,5,4096]{2,1,0:T(8,128)(2,1)S(1)} async-done(((bf16[8,5,4096]{2,1,0:T(8,128)(2,1)}), bf16[8,5,4096]{2,1,0:T(8,128)(2,1)S(1)}, u32[]{:S(2)}, u32[]{:S(2)}) %all-to-all-start.4) | async-done | bytes 327712 | tf_op jit(solution)/shard_map/while/body/eval_jaxpr/all_to_all | solution.py:94
  1027.7 5.2 all-to-all-done.5
  1056.5 21.3 %all_to_all.92 = bf16[8,5,4096]{2,1,0:T(8,128)(2,1)S(1)} all-to-all(bf16[8,5,4096]{2,1,0:T(8,128)(2,1)S(1)} %reshape.340), channel_id=1, replica_groups=mesh['pipe'=8,'tensor'=4,'expert'=8] {'expert'}, dimensions={0} | all-to-all | bytes 655360 | tf_op jit(solution)/shard_map/while/body/eval_jaxpr/all_to_all | solution.py:92
  1078.2 20.7 %all_to_all.93 = bf16[4,8,5,4096]{3,1,2,0:T(8,128)(2,1)S(1)} all-to-all(bf16[4,8,5,4096]{3,1,2,0:T(8,128)(2,1)S(1)} %broadcast_in_dim.48), channel_id=1, replica_groups=mesh['pipe'=8,'tensor'=4,'expert'=8] {'tensor'}, dimensions={0} | all-to-all | bytes 2621440 | tf_op jit(solution)/shard_map/while/body/eval_jaxpr/all_to_all | solution.py:11
  1113.8 17.0 %all-to-all-done.3 = bf16[4,8,5,4096]{3,1,2,0:T(8,128)(2,1)S(1)} async-done(((bf16[4,8,5,4096]{3,1,2,0:T(8,128)(2,1)}), bf16[4,8,5,4096]{3,1,2,0:T(8,128)(2,1)S(1)}, u32[]{:S(2)}, u32[]{:S(2)}) %all-to-all-start.3) | async-done | bytes 1310752 | tf_op jit(solution)/shard_map/while/body/eval_jaxpr/all_to_all | solution.py:32
  1136.5 14.2 %all-to-all-done.4 = bf16[8,5,4096]{2,1,0:T(8,128)(2,1)S(1)} async-done(((bf16[8,5,4096]{2,1,0:T(8,128)(2,1)}), bf16[8,5,4096]{2,1,0:T(8,128)(2,1)S(1)}, u32[]{:S(2)}, u32[]{:S(2)}) %all-to-all-start.4) | async-done | bytes 327712 | tf_op jit(solution)/shard_map/while/body/eval_jaxpr/all_to_all | solution.py:94
  1157.4 5.2 all-to-all-done.5
  (703 shorter events, 447.6 us)
Async XLA Ops:
  6.1 10.4 all-to-all-start
  16.6 24.8 %copy-start = (bf16[4,16,1024]{2,1,0:T(8,128)(2,1)}, bf16[4,16,1024]{2,1,0:T(8,128)(2,1)S(1)}, u32[]{:S(2)}) copy-start(bf16[4,16,1024]{2,1,0:T(8,128)(2,1)S(1)} %all-to-all-done) | copy-start | bytes 393220 | tf_op jit(solution)/shard_map/while
  73.3 20.6 %all-to-all-start.3 = ((bf16[4,8,5,4096]{3,1,2,0:T(8,128)(2,1)}), bf16[4,8,5,4096]{3,1,2,0:T(8,128)(2,1)S(1)}, u32[]{:S(2)}, u32[]{:S(2)}) async-start(bf16[4,8,5,4096]{3,1,2,0:T(8,128)(2,1)} %copy.62), calls=%async_computation.3 | async-start | bytes 2621440 | tf_op jit(solution)/shard_map/while/body/eval_jaxpr/all_to_all | solution.py:32
  95.2 21.5 %all-to-all-start.4 = ((bf16[8,5,4096]{2,1,0:T(8,128)(2,1)}), bf16[8,5,4096]{2,1,0:T(8,128)(2,1)S(1)}, u32[]{:S(2)}, u32[]{:S(2)}) async-start(bf16[8,5,4096]{2,1,0:T(8,128)(2,1)} %copy.63), calls=%async_computation.4 | async-start | bytes 1048576 | tf_op jit(solution)/shard_map/while/body/eval_jaxpr/all_to_all | solution.py:94
  119.3 9.3 all-to-all-start.5
  130.3 6.9 collective-permute-start
  142.0 9.3 all-to-all-start
  203.4 20.7 %all-to-all-start.3 = ((bf16[4,8,5,4096]{3,1,2,0:T(8,128)(2,1)}), bf16[4,8,5,4096]{3,1,2,0:T(8,128)(2,1)S(1)}, u32[]{:S(2)}, u32[]{:S(2)}) async-start(bf16[4,8,5,4096]{3,1,2,0:T(8,128)(2,1)} %copy.62), calls=%async_computation.3 | async-start | bytes 2621440 | tf_op jit(solution)/shard_map/while/body/eval_jaxpr/all_to_all | solution.py:32
  225.4 18.7 %all-to-all-start.4 = ((bf16[8,5,4096]{2,1,0:T(8,128)(2,1)}), bf16[8,5,4096]{2,1,0:T(8,128)(2,1)S(1)}, u32[]{:S(2)}, u32[]{:S(2)}) async-start(bf16[8,5,4096]{2,1,0:T(8,128)(2,1)} %copy.63), calls=%async_computation.4 | async-start | bytes 1048576 | tf_op jit(solution)/shard_map/while/body/eval_jaxpr/all_to_all | solution.py:94
  246.8 9.3 all-to-all-start.5
  257.8 7.5 collective-permute-start
  270.1 9.3 all-to-all-start
  331.7 20.7 %all-to-all-start.3 = ((bf16[4,8,5,4096]{3,1,2,0:T(8,128)(2,1)}), bf16[4,8,5,4096]{3,1,2,0:T(8,128)(2,1)S(1)}, u32[]{:S(2)}, u32[]{:S(2)}) async-start(bf16[4,8,5,4096]{3,1,2,0:T(8,128)(2,1)} %copy.62), calls=%async_computation.3 | async-start | bytes 2621440 | tf_op jit(solution)/shard_map/while/body/eval_jaxpr/all_to_all | solution.py:32
  353.7 18.6 %all-to-all-start.4 = ((bf16[8,5,4096]{2,1,0:T(8,128)(2,1)}), bf16[8,5,4096]{2,1,0:T(8,128)(2,1)S(1)}, u32[]{:S(2)}, u32[]{:S(2)}) async-start(bf16[8,5,4096]{2,1,0:T(8,128)(2,1)} %copy.63), calls=%async_computation.4 | async-start | bytes 1048576 | tf_op jit(solution)/shard_map/while/body/eval_jaxpr/all_to_all | solution.py:94
  375.0 9.3 all-to-all-start.5
  385.9 7.8 collective-permute-start
  398.5 9.3 all-to-all-start
  461.4 20.7 %all-to-all-start.3 = ((bf16[4,8,5,4096]{3,1,2,0:T(8,128)(2,1)}), bf16[4,8,5,4096]{3,1,2,0:T(8,128)(2,1)S(1)}, u32[]{:S(2)}, u32[]{:S(2)}) async-start(bf16[4,8,5,4096]{3,1,2,0:T(8,128)(2,1)} %copy.62), calls=%async_computation.3 | async-start | bytes 2621440 | tf_op jit(solution)/shard_map/while/body/eval_jaxpr/all_to_all | solution.py:32
  483.4 18.6 %all-to-all-start.4 = ((bf16[8,5,4096]{2,1,0:T(8,128)(2,1)}), bf16[8,5,4096]{2,1,0:T(8,128)(2,1)S(1)}, u32[]{:S(2)}, u32[]{:S(2)}) async-start(bf16[8,5,4096]{2,1,0:T(8,128)(2,1)} %copy.63), calls=%async_computation.4 | async-start | bytes 1048576 | tf_op jit(solution)/shard_map/while/body/eval_jaxpr/all_to_all | solution.py:94
  504.7 9.3 all-to-all-start.5
  515.6 6.9 collective-permute-start
  527.3 9.3 all-to-all-start
  536.6 22.4 %copy-start = (bf16[4,16,1024]{2,1,0:T(8,128)(2,1)}, bf16[4,16,1024]{2,1,0:T(8,128)(2,1)S(1)}, u32[]{:S(2)}) copy-start(bf16[4,16,1024]{2,1,0:T(8,128)(2,1)S(1)} %all-to-all-done) | copy-start | bytes 393220 | tf_op jit(solution)/shard_map/while
  591.1 20.7 %all-to-all-start.3 = ((bf16[4,8,5,4096]{3,1,2,0:T(8,128)(2,1)}), bf16[4,8,5,4096]{3,1,2,0:T(8,128)(2,1)S(1)}, u32[]{:S(2)}, u32[]{:S(2)}) async-start(bf16[4,8,5,4096]{3,1,2,0:T(8,128)(2,1)} %copy.62), calls=%async_computation.3 | async-start | bytes 2621440 | tf_op jit(solution)/shard_map/while/body/eval_jaxpr/all_to_all | solution.py:32
  613.1 18.6 %all-to-all-start.4 = ((bf16[8,5,4096]{2,1,0:T(8,128)(2,1)}), bf16[8,5,4096]{2,1,0:T(8,128)(2,1)S(1)}, u32[]{:S(2)}, u32[]{:S(2)}) async-start(bf16[8,5,4096]{2,1,0:T(8,128)(2,1)} %copy.63), calls=%async_computation.4 | async-start | bytes 1048576 | tf_op jit(solution)/shard_map/while/body/eval_jaxpr/all_to_all | solution.py:94
  634.4 9.3 all-to-all-start.5
  645.4 6.9 collective-permute-start
  657.1 9.3 all-to-all-start
  720.9 20.7 %all-to-all-start.3 = ((bf16[4,8,5,4096]{3,1,2,0:T(8,128)(2,1)}), bf16[4,8,5,4096]{3,1,2,0:T(8,128)(2,1)S(1)}, u32[]{:S(2)}, u32[]{:S(2)}) async-start(bf16[4,8,5,4096]{3,1,2,0:T(8,128)(2,1)} %copy.62), calls=%async_computation.3 | async-start | bytes 2621440 | tf_op jit(solution)/shard_map/while/body/eval_jaxpr/all_to_all | solution.py:32
  742.9 18.6 %all-to-all-start.4 = ((bf16[8,5,4096]{2,1,0:T(8,128)(2,1)}), bf16[8,5,4096]{2,1,0:T(8,128)(2,1)S(1)}, u32[]{:S(2)}, u32[]{:S(2)}) async-start(bf16[8,5,4096]{2,1,0:T(8,128)(2,1)} %copy.63), calls=%async_computation.4 | async-start | bytes 1048576 | tf_op jit(solution)/shard_map/while/body/eval_jaxpr/all_to_all | solution.py:94
  764.1 9.3 all-to-all-start.5
  775.1 6.9 collective-permute-start
  786.8 9.3 all-to-all-start
  850.6 20.7 %all-to-all-start.3 = ((bf16[4,8,5,4096]{3,1,2,0:T(8,128)(2,1)}), bf16[4,8,5,4096]{3,1,2,0:T(8,128)(2,1)S(1)}, u32[]{:S(2)}, u32[]{:S(2)}) async-start(bf16[4,8,5,4096]{3,1,2,0:T(8,128)(2,1)} %copy.62), calls=%async_computation.3 | async-start | bytes 2621440 | tf_op jit(solution)/shard_map/while/body/eval_jaxpr/all_to_all | solution.py:32
  872.6 18.6 %all-to-all-start.4 = ((bf16[8,5,4096]{2,1,0:T(8,128)(2,1)}), bf16[8,5,4096]{2,1,0:T(8,128)(2,1)S(1)}, u32[]{:S(2)}, u32[]{:S(2)}) async-start(bf16[8,5,4096]{2,1,0:T(8,128)(2,1)} %copy.63), calls=%async_computation.4 | async-start | bytes 1048576 | tf_op jit(solution)/shard_map/while/body/eval_jaxpr/all_to_all | solution.py:94
  893.9 9.3 all-to-all-start.5
  904.8 6.9 collective-permute-start
  916.5 9.3 all-to-all-start
  925.8 22.4 %copy-start = (bf16[4,16,1024]{2,1,0:T(8,128)(2,1)}, bf16[4,16,1024]{2,1,0:T(8,128)(2,1)S(1)}, u32[]{:S(2)}) copy-start(bf16[4,16,1024]{2,1,0:T(8,128)(2,1)S(1)} %all-to-all-done) | copy-start | bytes 393220 | tf_op jit(solution)/shard_map/while
  980.3 20.7 %all-to-all-start.3 = ((bf16[4,8,5,4096]{3,1,2,0:T(8,128)(2,1)}), bf16[4,8,5,4096]{3,1,2,0:T(8,128)(2,1)S(1)}, u32[]{:S(2)}, u32[]{:S(2)}) async-start(bf16[4,8,5,4096]{3,1,2,0:T(8,128)(2,1)} %copy.62), calls=%async_computation.3 | async-start | bytes 2621440 | tf_op jit(solution)/shard_map/while/body/eval_jaxpr/all_to_all | solution.py:32
  1002.3 18.6 %all-to-all-start.4 = ((bf16[8,5,4096]{2,1,0:T(8,128)(2,1)}), bf16[8,5,4096]{2,1,0:T(8,128)(2,1)S(1)}, u32[]{:S(2)}, u32[]{:S(2)}) async-start(bf16[8,5,4096]{2,1,0:T(8,128)(2,1)} %copy.63), calls=%async_computation.4 | async-start | bytes 1048576 | tf_op jit(solution)/shard_map/while/body/eval_jaxpr/all_to_all | solution.py:94
  1023.6 9.3 all-to-all-start.5
  1034.5 6.9 collective-permute-start
  1046.2 9.3 all-to-all-start
  1110.0 20.7 %all-to-all-start.3 = ((bf16[4,8,5,4096]{3,1,2,0:T(8,128)(2,1)}), bf16[4,8,5,4096]{3,1,2,0:T(8,128)(2,1)S(1)}, u32[]{:S(2)}, u32[]{:S(2)}) async-start(bf16[4,8,5,4096]{3,1,2,0:T(8,128)(2,1)} %copy.62), calls=%async_computation.3 | async-start | bytes 2621440 | tf_op jit(solution)/shard_map/while/body/eval_jaxpr/all_to_all | solution.py:32
  1132.0 18.6 %all-to-all-start.4 = ((bf16[8,5,4096]{2,1,0:T(8,128)(2,1)}), bf16[8,5,4096]{2,1,0:T(8,128)(2,1)S(1)}, u32[]{:S(2)}, u32[]{:S(2)}) async-start(bf16[8,5,4096]{2,1,0:T(8,128)(2,1)} %copy.63), calls=%async_computation.4 | async-start | bytes 1048576 | tf_op jit(solution)/shard_map/while/body/eval_jaxpr/all_to_all | solution.py:94
  1153.3 9.3 all-to-all-start.5
  1164.3 6.9 collective-permute-start
  (78 other events, 767.5 us)
where the time goes:
time: 1180 us; the launch traced here: 1170 us
  waiting for transfers between devices  396 us (34%)
  blocking collectives  375 us (32%)
  starting transfers between devices  154 us (13%)
  local copies, waits for them, and re-layouts  115 us (10%)
  matrix products  67.2 us (6%)
  other arithmetic  56.2 us (5%)
    all_to_all x9, blocking collectives, expert_layer(): lax.all_to_all(outgoing, 'expert', split_axis=0, concat_axis=0, tiled=True)  189 us
    all_to_all x9, blocking collectives, from_everyone(): return lax.all_to_all(copies, axis, split_axis=0, concat_axis=0, tiled=True)  186 us
    all_to_all x9, waiting for transfers between devices, sum_at_owner(): lax.all_to_all(pieces, axis, split_axis=0, concat_axis=0, tiled=True)  153 us
    all_to_all x9, waiting for transfers between devices, expert_layer(): lax.all_to_all(returned, 'expert', split_axis=0, concat_axis=0, tiled=True)  130 us
    all_to_all x9, waiting for transfers between devices, run_section(): lax.all_to_all(fresh_rows, 'tensor', split_axis=1, concat_axis=0, tiled=T...  46.4 us
    dot_general x9, matrix products, expert_work(): jnp.dot(hidden, down_matrix, preferred_element_type=jnp.float32)  40.5 us
    ppermute x9, waiting for transfers between devices, passed_along(): return lax.ppermute(block, axis, route)  35 us
    all_to_all x9, starting transfers between devices, sum_at_owner(): lax.all_to_all(pieces, axis, split_axis=0, concat_axis=0, tiled=True)  33 us
  transfers between devices with their start and end apart: 45, of which 45 were waited for; matrix products, arithmetic and copies ran while one was open for 3% of the time, Pallas kernels for 0%

commit v1 on v0

--- a/solution.py
+++ b/solution.py
@@ -4,6 +4,19 @@
 from jax.sharding import PartitionSpec as P
 
 epsilon = 1e-06
+
+
+def register_map(vals, where_dim, q_in):
+    y1, local_out = (vals.shape[:where_dim], vals.shape[where_dim + 1 :])
+    return jnp.moveaxis(vals.reshape(*y1, q_in, -1, *local_out), where_dim, 0)
+
+
+def waves_hold(tile_in, dim_at):
+    tile_in = jnp.moveaxis(tile_in, 0, dim_at)
+    arr_now = tile_in.shape
+    return tile_in.reshape(
+        *arr_now[:dim_at], arr_now[dim_at] * arr_now[dim_at + 1], *arr_now[dim_at + 2 :]
+    )
 
 
 def from_everyone(value, axis):
@@ -109,7 +122,18 @@
         order_all = picks[0, micro_index, 0]
         chosen = lax.dynamic_slice_in_dim(order_all, my_rank * quarter, quarter)
         permuted = stream[order_all]
-        quarter_rows = lax.all_to_all(permuted, "tensor", split_axis=0, concat_axis=1, tiled=True)
+        lower, raw_out = (lax.axis_size("tensor"), lax.axis_index("tensor"))
+        x_next = register_map(permuted, 0, lower)
+        chunks = [x_next[raw_out]]
+        for h in range(1, lower):
+            long_array = x_next[raw_out ^ h]
+            chunks.append(
+                lax.ppermute(
+                    long_array, axis_name="tensor", perm=[(k, k ^ h) for k in range(lower)]
+                )
+            )
+        x_next = jnp.stack(chunks)[raw_out ^ jnp.arange(lower)]
+        quarter_rows = waves_hold(x_next, 1)
         fresh_rows = expert_layer(quarter_rows, chosen, micro_index)
         spread = lax.all_to_all(fresh_rows, "tensor", split_axis=1, concat_axis=0, tiled=True)
         return jnp.zeros_like(stream).at[order_all].set(spread)

time: 1180 us -> 1160 us (0.983)
  waiting for transfers between devices: 396 us -> 368 us
    ppermute x0 -> x27, starting transfers between devices: none -> 37.6 us  [run_section(): lax.ppermute(long_array, axis_name='tensor', perm=[(k, k ^ h) for k in ra...]
    all_to_all x9 -> x0, starting transfers between devices: 31 us -> none  [run_section(): lax.all_to_all(permuted, 'tensor', split_axis=0, concat_axis=1, tiled=True)]
    all_to_all x9 -> x0, waiting for transfers between devices: 31 us -> none  [run_section(): lax.all_to_all(permuted, 'tensor', split_axis=0, concat_axis=1, tiled=True)]
  transfers between devices with their start and end apart: 45 -> 63, of which waited for: 45 -> 37; matrix products, arithmetic and copies ran while one was open for 3% -> 3% of each run, Pallas kernels for 0% -> 0%
where the time goes in v1:
time: 1160 us; the launch traced here: 1150 us
  blocking collectives  378 us (33%)
  waiting for transfers between devices  368 us (32%)
  starting transfers between devices  156 us (13%)
  local copies, waits for them, and re-layouts  119 us (10%)
  matrix products  67.2 us (6%)
  other arithmetic  55.5 us (5%)
    all_to_all x9, blocking collectives, expert_layer(): lax.all_to_all(outgoing, 'expert', split_axis=0, concat_axis=0, tiled=True)  191 us
    all_to_all x9, blocking collectives, from_everyone(): return lax.all_to_all(copies, axis, split_axis=0, concat_axis=0, tiled=True)  186 us
    all_to_all x9, waiting for transfers between devices, sum_at_owner(): lax.all_to_all(pieces, axis, split_axis=0, concat_axis=0, tiled=True)  151 us
    all_to_all x9, waiting for transfers between devices, expert_layer(): lax.all_to_all(returned, 'expert', split_axis=0, concat_axis=0, tiled=True)  130 us
    all_to_all x9, waiting for transfers between devices, run_section(): lax.all_to_all(fresh_rows, 'tensor', split_axis=1, concat_axis=0, tiled=T...  46.8 us
    dot_general x9, matrix products, expert_work(): jnp.dot(hidden, down_matrix, preferred_element_type=jnp.float32)  40.5 us
    ppermute x9, waiting for transfers between devices, passed_along(): return lax.ppermute(block, axis, route)  37.8 us
    ppermute x27, starting transfers between devices, run_section(): lax.ppermute(long_array, axis_name='tensor', perm=[(k, k ^ h) for k in ra...  37.6 us
  transfers between devices with their start and end apart: 63, of which 37 were waited for; matrix products, arithmetic and copies ran while one was open for 3% of the time, Pallas kernels for 0%

profile of v1, /device:TPU:32, one launch (start us, length us, event | category | flops | bytes accessed | tf_op | source)
XLA Modules:
  0.0 1153.7 jit_solution(14323589501952192600)
XLA Ops:
  1.3 1152.4 %while.16 = (s32[]{:T(128)}, bf16[64,1024]{1,0:T(8,128)(2,1)S(1)}, bf16[2,64,1024]{2,1,0:T(8,128)(2,1)}, s32[9]{0:T(128)}, s32[]{:T(128)}, /*index=5*/s32[1,2,1,...) while((s32[]{:T(128)}, bf16[64,1024]{1,0:T(8,128)(2,1)S(1)}, ...), condition=%wide.region_8.9_spmd, body=%wide.region_0.8_spmd.sunk | while | flops 1523440896 | bytes 51867752 | solution.py:163
  15.8 23.8 %all_to_all.67 = bf16[8,5,4096]{2,1,0:T(8,128)(2,1)S(1)} all-to-all(bf16[8,5,4096]{2,1,0:T(8,128)(2,1)S(1)} %reshape.373), channel_id=1, replica_groups=mesh['pipe'=8,'tensor'=4,'expert'=8] {'expert'}, dimensions={0} | all-to-all | bytes 655360 | tf_op jit(solution)/shard_map/while/body/eval_jaxpr/all_to_all | solution.py:105
  39.9 20.8 %all_to_all.68 = bf16[4,8,5,4096]{3,1,2,0:T(8,128)(2,1)S(1)} all-to-all(bf16[4,8,5,4096]{3,1,2,0:T(8,128)(2,1)S(1)} %broadcast_in_dim.49), channel_id=1, replica_groups=mesh['pipe'=8,'tensor'=4,'expert'=8] {'tensor'}, dimensions={0} | all-to-all | bytes 2621440 | tf_op jit(solution)/shard_map/while/body/eval_jaxpr/all_to_all | solution.py:24
  75.6 16.8 %all-to-all-done.2 = bf16[4,8,5,4096]{3,1,2,0:T(8,128)(2,1)S(1)} async-done(((bf16[4,8,5,4096]{3,1,2,0:T(8,128)(2,1)}), bf16[4,8,5,4096]{3,1,2,0:T(8,128)(2,1)S(1)}, u32[]{:S(2)}, u32[]{:S(2)}) %all-to-all-start.2) | async-done | bytes 1310752 | tf_op jit(solution)/shard_map/while/body/eval_jaxpr/all_to_all | solution.py:45
  98.1 16.9 %all-to-all-done.3 = bf16[8,5,4096]{2,1,0:T(8,128)(2,1)S(1)} async-done(((bf16[8,5,4096]{2,1,0:T(8,128)(2,1)}), bf16[8,5,4096]{2,1,0:T(8,128)(2,1)S(1)}, u32[]{:S(2)}, u32[]{:S(2)}) %all-to-all-start.3) | async-done | bytes 327712 | tf_op jit(solution)/shard_map/while/body/eval_jaxpr/all_to_all | solution.py:107
  121.8 5.2 all-to-all-done.4
  148.7 18.9 %all_to_all.67 = bf16[8,5,4096]{2,1,0:T(8,128)(2,1)S(1)} all-to-all(bf16[8,5,4096]{2,1,0:T(8,128)(2,1)S(1)} %reshape.373), channel_id=1, replica_groups=mesh['pipe'=8,'tensor'=4,'expert'=8] {'expert'}, dimensions={0} | all-to-all | bytes 655360 | tf_op jit(solution)/shard_map/while/body/eval_jaxpr/all_to_all | solution.py:105
  168.0 20.7 %all_to_all.68 = bf16[4,8,5,4096]{3,1,2,0:T(8,128)(2,1)S(1)} all-to-all(bf16[4,8,5,4096]{3,1,2,0:T(8,128)(2,1)S(1)} %broadcast_in_dim.49), channel_id=1, replica_groups=mesh['pipe'=8,'tensor'=4,'expert'=8] {'tensor'}, dimensions={0} | all-to-all | bytes 2621440 | tf_op jit(solution)/shard_map/while/body/eval_jaxpr/all_to_all | solution.py:24
  203.6 16.8 %all-to-all-done.2 = bf16[4,8,5,4096]{3,1,2,0:T(8,128)(2,1)S(1)} async-done(((bf16[4,8,5,4096]{3,1,2,0:T(8,128)(2,1)}), bf16[4,8,5,4096]{3,1,2,0:T(8,128)(2,1)S(1)}, u32[]{:S(2)}, u32[]{:S(2)}) %all-to-all-start.2) | async-done | bytes 1310752 | tf_op jit(solution)/shard_map/while/body/eval_jaxpr/all_to_all | solution.py:45
  226.1 14.3 %all-to-all-done.3 = bf16[8,5,4096]{2,1,0:T(8,128)(2,1)S(1)} async-done(((bf16[8,5,4096]{2,1,0:T(8,128)(2,1)}), bf16[8,5,4096]{2,1,0:T(8,128)(2,1)S(1)}, u32[]{:S(2)}, u32[]{:S(2)}) %all-to-all-start.3) | async-done | bytes 327712 | tf_op jit(solution)/shard_map/while/body/eval_jaxpr/all_to_all | solution.py:107
  247.1 5.2 all-to-all-done.4
  254.0 5.0 collective-permute-start.3
  274.6 20.6 %all_to_all.67 = bf16[8,5,4096]{2,1,0:T(8,128)(2,1)S(1)} all-to-all(bf16[8,5,4096]{2,1,0:T(8,128)(2,1)S(1)} %reshape.373), channel_id=1, replica_groups=mesh['pipe'=8,'tensor'=4,'expert'=8] {'expert'}, dimensions={0} | all-to-all | bytes 655360 | tf_op jit(solution)/shard_map/while/body/eval_jaxpr/all_to_all | solution.py:105
  295.5 20.7 %all_to_all.68 = bf16[4,8,5,4096]{3,1,2,0:T(8,128)(2,1)S(1)} all-to-all(bf16[4,8,5,4096]{3,1,2,0:T(8,128)(2,1)S(1)} %broadcast_in_dim.49), channel_id=1, replica_groups=mesh['pipe'=8,'tensor'=4,'expert'=8] {'tensor'}, dimensions={0} | all-to-all | bytes 2621440 | tf_op jit(solution)/shard_map/while/body/eval_jaxpr/all_to_all | solution.py:24
  331.1 16.8 %all-to-all-done.2 = bf16[4,8,5,4096]{3,1,2,0:T(8,128)(2,1)S(1)} async-done(((bf16[4,8,5,4096]{3,1,2,0:T(8,128)(2,1)}), bf16[4,8,5,4096]{3,1,2,0:T(8,128)(2,1)S(1)}, u32[]{:S(2)}, u32[]{:S(2)}) %all-to-all-start.2) | async-done | bytes 1310752 | tf_op jit(solution)/shard_map/while/body/eval_jaxpr/all_to_all | solution.py:45
  353.7 14.1 %all-to-all-done.3 = bf16[8,5,4096]{2,1,0:T(8,128)(2,1)S(1)} async-done(((bf16[8,5,4096]{2,1,0:T(8,128)(2,1)}), bf16[8,5,4096]{2,1,0:T(8,128)(2,1)S(1)}, u32[]{:S(2)}, u32[]{:S(2)}) %all-to-all-start.3) | async-done | bytes 327712 | tf_op jit(solution)/shard_map/while/body/eval_jaxpr/all_to_all | solution.py:107
  374.6 5.2 all-to-all-done.4
  401.4 21.3 %all_to_all.67 = bf16[8,5,4096]{2,1,0:T(8,128)(2,1)S(1)} all-to-all(bf16[8,5,4096]{2,1,0:T(8,128)(2,1)S(1)} %reshape.373), channel_id=1, replica_groups=mesh['pipe'=8,'tensor'=4,'expert'=8] {'expert'}, dimensions={0} | all-to-all | bytes 655360 | tf_op jit(solution)/shard_map/while/body/eval_jaxpr/all_to_all | solution.py:105
  423.1 20.7 %all_to_all.68 = bf16[4,8,5,4096]{3,1,2,0:T(8,128)(2,1)S(1)} all-to-all(bf16[4,8,5,4096]{3,1,2,0:T(8,128)(2,1)S(1)} %broadcast_in_dim.49), channel_id=1, replica_groups=mesh['pipe'=8,'tensor'=4,'expert'=8] {'tensor'}, dimensions={0} | all-to-all | bytes 2621440 | tf_op jit(solution)/shard_map/while/body/eval_jaxpr/all_to_all | solution.py:24
  458.7 16.8 %all-to-all-done.2 = bf16[4,8,5,4096]{3,1,2,0:T(8,128)(2,1)S(1)} async-done(((bf16[4,8,5,4096]{3,1,2,0:T(8,128)(2,1)}), bf16[4,8,5,4096]{3,1,2,0:T(8,128)(2,1)S(1)}, u32[]{:S(2)}, u32[]{:S(2)}) %all-to-all-start.2) | async-done | bytes 1310752 | tf_op jit(solution)/shard_map/while/body/eval_jaxpr/all_to_all | solution.py:45
  481.2 14.1 %all-to-all-done.3 = bf16[8,5,4096]{2,1,0:T(8,128)(2,1)S(1)} async-done(((bf16[8,5,4096]{2,1,0:T(8,128)(2,1)}), bf16[8,5,4096]{2,1,0:T(8,128)(2,1)S(1)}, u32[]{:S(2)}, u32[]{:S(2)}) %all-to-all-start.3) | async-done | bytes 327712 | tf_op jit(solution)/shard_map/while/body/eval_jaxpr/all_to_all | solution.py:107
  502.1 5.2 all-to-all-done.4
  529.0 21.3 %all_to_all.67 = bf16[8,5,4096]{2,1,0:T(8,128)(2,1)S(1)} all-to-all(bf16[8,5,4096]{2,1,0:T(8,128)(2,1)S(1)} %reshape.373), channel_id=1, replica_groups=mesh['pipe'=8,'tensor'=4,'expert'=8] {'expert'}, dimensions={0} | all-to-all | bytes 655360 | tf_op jit(solution)/shard_map/while/body/eval_jaxpr/all_to_all | solution.py:105
  550.7 20.7 %all_to_all.68 = bf16[4,8,5,4096]{3,1,2,0:T(8,128)(2,1)S(1)} all-to-all(bf16[4,8,5,4096]{3,1,2,0:T(8,128)(2,1)S(1)} %broadcast_in_dim.49), channel_id=1, replica_groups=mesh['pipe'=8,'tensor'=4,'expert'=8] {'tensor'}, dimensions={0} | all-to-all | bytes 2621440 | tf_op jit(solution)/shard_map/while/body/eval_jaxpr/all_to_all | solution.py:24
  586.3 16.8 %all-to-all-done.2 = bf16[4,8,5,4096]{3,1,2,0:T(8,128)(2,1)S(1)} async-done(((bf16[4,8,5,4096]{3,1,2,0:T(8,128)(2,1)}), bf16[4,8,5,4096]{3,1,2,0:T(8,128)(2,1)S(1)}, u32[]{:S(2)}, u32[]{:S(2)}) %all-to-all-start.2) | async-done | bytes 1310752 | tf_op jit(solution)/shard_map/while/body/eval_jaxpr/all_to_all | solution.py:45
  608.8 14.1 %all-to-all-done.3 = bf16[8,5,4096]{2,1,0:T(8,128)(2,1)S(1)} async-done(((bf16[8,5,4096]{2,1,0:T(8,128)(2,1)}), bf16[8,5,4096]{2,1,0:T(8,128)(2,1)S(1)}, u32[]{:S(2)}, u32[]{:S(2)}) %all-to-all-start.3) | async-done | bytes 327712 | tf_op jit(solution)/shard_map/while/body/eval_jaxpr/all_to_all | solution.py:107
  629.7 5.2 all-to-all-done.4
  656.6 21.3 %all_to_all.67 = bf16[8,5,4096]{2,1,0:T(8,128)(2,1)S(1)} all-to-all(bf16[8,5,4096]{2,1,0:T(8,128)(2,1)S(1)} %reshape.373), channel_id=1, replica_groups=mesh['pipe'=8,'tensor'=4,'expert'=8] {'expert'}, dimensions={0} | all-to-all | bytes 655360 | tf_op jit(solution)/shard_map/while/body/eval_jaxpr/all_to_all | solution.py:105
  678.3 20.7 %all_to_all.68 = bf16[4,8,5,4096]{3,1,2,0:T(8,128)(2,1)S(1)} all-to-all(bf16[4,8,5,4096]{3,1,2,0:T(8,128)(2,1)S(1)} %broadcast_in_dim.49), channel_id=1, replica_groups=mesh['pipe'=8,'tensor'=4,'expert'=8] {'tensor'}, dimensions={0} | all-to-all | bytes 2621440 | tf_op jit(solution)/shard_map/while/body/eval_jaxpr/all_to_all | solution.py:24
  713.8 16.8 %all-to-all-done.2 = bf16[4,8,5,4096]{3,1,2,0:T(8,128)(2,1)S(1)} async-done(((bf16[4,8,5,4096]{3,1,2,0:T(8,128)(2,1)}), bf16[4,8,5,4096]{3,1,2,0:T(8,128)(2,1)S(1)}, u32[]{:S(2)}, u32[]{:S(2)}) %all-to-all-start.2) | async-done | bytes 1310752 | tf_op jit(solution)/shard_map/while/body/eval_jaxpr/all_to_all | solution.py:45
  736.4 14.1 %all-to-all-done.3 = bf16[8,5,4096]{2,1,0:T(8,128)(2,1)S(1)} async-done(((bf16[8,5,4096]{2,1,0:T(8,128)(2,1)}), bf16[8,5,4096]{2,1,0:T(8,128)(2,1)S(1)}, u32[]{:S(2)}, u32[]{:S(2)}) %all-to-all-start.3) | async-done | bytes 327712 | tf_op jit(solution)/shard_map/while/body/eval_jaxpr/all_to_all | solution.py:107
  757.3 5.2 all-to-all-done.4
  766.0 4.9 collective-permute-done.3
  784.1 21.3 %all_to_all.67 = bf16[8,5,4096]{2,1,0:T(8,128)(2,1)S(1)} all-to-all(bf16[8,5,4096]{2,1,0:T(8,128)(2,1)S(1)} %reshape.373), channel_id=1, replica_groups=mesh['pipe'=8,'tensor'=4,'expert'=8] {'expert'}, dimensions={0} | all-to-all | bytes 655360 | tf_op jit(solution)/shard_map/while/body/eval_jaxpr/all_to_all | solution.py:105
  805.8 20.7 %all_to_all.68 = bf16[4,8,5,4096]{3,1,2,0:T(8,128)(2,1)S(1)} all-to-all(bf16[4,8,5,4096]{3,1,2,0:T(8,128)(2,1)S(1)} %broadcast_in_dim.49), channel_id=1, replica_groups=mesh['pipe'=8,'tensor'=4,'expert'=8] {'tensor'}, dimensions={0} | all-to-all | bytes 2621440 | tf_op jit(solution)/shard_map/while/body/eval_jaxpr/all_to_all | solution.py:24
  841.4 16.8 %all-to-all-done.2 = bf16[4,8,5,4096]{3,1,2,0:T(8,128)(2,1)S(1)} async-done(((bf16[4,8,5,4096]{3,1,2,0:T(8,128)(2,1)}), bf16[4,8,5,4096]{3,1,2,0:T(8,128)(2,1)S(1)}, u32[]{:S(2)}, u32[]{:S(2)}) %all-to-all-start.2) | async-done | bytes 1310752 | tf_op jit(solution)/shard_map/while/body/eval_jaxpr/all_to_all | solution.py:45
  863.9 14.1 %all-to-all-done.3 = bf16[8,5,4096]{2,1,0:T(8,128)(2,1)S(1)} async-done(((bf16[8,5,4096]{2,1,0:T(8,128)(2,1)}), bf16[8,5,4096]{2,1,0:T(8,128)(2,1)S(1)}, u32[]{:S(2)}, u32[]{:S(2)}) %all-to-all-start.3) | async-done | bytes 327712 | tf_op jit(solution)/shard_map/while/body/eval_jaxpr/all_to_all | solution.py:107
  884.8 5.2 all-to-all-done.4
  911.7 21.3 %all_to_all.67 = bf16[8,5,4096]{2,1,0:T(8,128)(2,1)S(1)} all-to-all(bf16[8,5,4096]{2,1,0:T(8,128)(2,1)S(1)} %reshape.373), channel_id=1, replica_groups=mesh['pipe'=8,'tensor'=4,'expert'=8] {'expert'}, dimensions={0} | all-to-all | bytes 655360 | tf_op jit(solution)/shard_map/while/body/eval_jaxpr/all_to_all | solution.py:105
  933.4 20.7 %all_to_all.68 = bf16[4,8,5,4096]{3,1,2,0:T(8,128)(2,1)S(1)} all-to-all(bf16[4,8,5,4096]{3,1,2,0:T(8,128)(2,1)S(1)} %broadcast_in_dim.49), channel_id=1, replica_groups=mesh['pipe'=8,'tensor'=4,'expert'=8] {'tensor'}, dimensions={0} | all-to-all | bytes 2621440 | tf_op jit(solution)/shard_map/while/body/eval_jaxpr/all_to_all | solution.py:24
  969.0 16.8 %all-to-all-done.2 = bf16[4,8,5,4096]{3,1,2,0:T(8,128)(2,1)S(1)} async-done(((bf16[4,8,5,4096]{3,1,2,0:T(8,128)(2,1)}), bf16[4,8,5,4096]{3,1,2,0:T(8,128)(2,1)S(1)}, u32[]{:S(2)}, u32[]{:S(2)}) %all-to-all-start.2) | async-done | bytes 1310752 | tf_op jit(solution)/shard_map/while/body/eval_jaxpr/all_to_all | solution.py:45
  991.5 14.1 %all-to-all-done.3 = bf16[8,5,4096]{2,1,0:T(8,128)(2,1)S(1)} async-done(((bf16[8,5,4096]{2,1,0:T(8,128)(2,1)}), bf16[8,5,4096]{2,1,0:T(8,128)(2,1)S(1)}, u32[]{:S(2)}, u32[]{:S(2)}) %all-to-all-start.3) | async-done | bytes 327712 | tf_op jit(solution)/shard_map/while/body/eval_jaxpr/all_to_all | solution.py:107
  1012.4 5.2 all-to-all-done.4
  1039.3 21.3 %all_to_all.67 = bf16[8,5,4096]{2,1,0:T(8,128)(2,1)S(1)} all-to-all(bf16[8,5,4096]{2,1,0:T(8,128)(2,1)S(1)} %reshape.373), channel_id=1, replica_groups=mesh['pipe'=8,'tensor'=4,'expert'=8] {'expert'}, dimensions={0} | all-to-all | bytes 655360 | tf_op jit(solution)/shard_map/while/body/eval_jaxpr/all_to_all | solution.py:105
  1061.0 20.7 %all_to_all.68 = bf16[4,8,5,4096]{3,1,2,0:T(8,128)(2,1)S(1)} all-to-all(bf16[4,8,5,4096]{3,1,2,0:T(8,128)(2,1)S(1)} %broadcast_in_dim.49), channel_id=1, replica_groups=mesh['pipe'=8,'tensor'=4,'expert'=8] {'tensor'}, dimensions={0} | all-to-all | bytes 2621440 | tf_op jit(solution)/shard_map/while/body/eval_jaxpr/all_to_all | solution.py:24
  1096.5 16.8 %all-to-all-done.2 = bf16[4,8,5,4096]{3,1,2,0:T(8,128)(2,1)S(1)} async-done(((bf16[4,8,5,4096]{3,1,2,0:T(8,128)(2,1)}), bf16[4,8,5,4096]{3,1,2,0:T(8,128)(2,1)S(1)}, u32[]{:S(2)}, u32[]{:S(2)}) %all-to-all-start.2) | async-done | bytes 1310752 | tf_op jit(solution)/shard_map/while/body/eval_jaxpr/all_to_all | solution.py:45
  1119.1 14.1 %all-to-all-done.3 = bf16[8,5,4096]{2,1,0:T(8,128)(2,1)S(1)} async-done(((bf16[8,5,4096]{2,1,0:T(8,128)(2,1)}), bf16[8,5,4096]{2,1,0:T(8,128)(2,1)S(1)}, u32[]{:S(2)}, u32[]{:S(2)}) %all-to-all-start.3) | async-done | bytes 327712 | tf_op jit(solution)/shard_map/while/body/eval_jaxpr/all_to_all | solution.py:107
  1140.0 5.2 all-to-all-done.4
  (784 shorter events, 428.2 us)
Async XLA Ops:
  5.7 6.7 collective-permute-start
  71.9 20.5 %all-to-all-start.2 = ((bf16[4,8,5,4096]{3,1,2,0:T(8,128)(2,1)}), bf16[4,8,5,4096]{3,1,2,0:T(8,128)(2,1)S(1)}, u32[]{:S(2)}, u32[]{:S(2)}) async-start(bf16[4,8,5,4096]{3,1,2,0:T(8,128)(2,1)} %copy.57), calls=%async_computation.2 | async-start | bytes 2621440 | tf_op jit(solution)/shard_map/while/body/eval_jaxpr/all_to_all | solution.py:45
  93.7 21.4 %all-to-all-start.3 = ((bf16[8,5,4096]{2,1,0:T(8,128)(2,1)}), bf16[8,5,4096]{2,1,0:T(8,128)(2,1)S(1)}, u32[]{:S(2)}, u32[]{:S(2)}) async-start(bf16[8,5,4096]{2,1,0:T(8,128)(2,1)} %copy.58), calls=%async_computation.3 | async-start | bytes 1048576 | tf_op jit(solution)/shard_map/while/body/eval_jaxpr/all_to_all | solution.py:107
  117.7 9.3 all-to-all-start.4
  128.6 6.9 collective-permute-start.3
  139.8 6.7 collective-permute-start
  141.1 5.5 collective-permute-start.1
  199.8 20.6 %all-to-all-start.2 = ((bf16[4,8,5,4096]{3,1,2,0:T(8,128)(2,1)}), bf16[4,8,5,4096]{3,1,2,0:T(8,128)(2,1)S(1)}, u32[]{:S(2)}, u32[]{:S(2)}) async-start(bf16[4,8,5,4096]{3,1,2,0:T(8,128)(2,1)} %copy.57), calls=%async_computation.2 | async-start | bytes 2621440 | tf_op jit(solution)/shard_map/while/body/eval_jaxpr/all_to_all | solution.py:45
  221.7 18.7 %all-to-all-start.3 = ((bf16[8,5,4096]{2,1,0:T(8,128)(2,1)}), bf16[8,5,4096]{2,1,0:T(8,128)(2,1)S(1)}, u32[]{:S(2)}, u32[]{:S(2)}) async-start(bf16[8,5,4096]{2,1,0:T(8,128)(2,1)} %copy.58), calls=%async_computation.3 | async-start | bytes 1048576 | tf_op jit(solution)/shard_map/while/body/eval_jaxpr/all_to_all | solution.py:107
  243.1 9.3 all-to-all-start.4
  254.0 7.5 collective-permute-start.3
  265.8 6.7 collective-permute-start
  327.4 20.6 %all-to-all-start.2 = ((bf16[4,8,5,4096]{3,1,2,0:T(8,128)(2,1)}), bf16[4,8,5,4096]{3,1,2,0:T(8,128)(2,1)S(1)}, u32[]{:S(2)}, u32[]{:S(2)}) async-start(bf16[4,8,5,4096]{3,1,2,0:T(8,128)(2,1)} %copy.57), calls=%async_computation.2 | async-start | bytes 2621440 | tf_op jit(solution)/shard_map/while/body/eval_jaxpr/all_to_all | solution.py:45
  349.2 18.6 %all-to-all-start.3 = ((bf16[8,5,4096]{2,1,0:T(8,128)(2,1)}), bf16[8,5,4096]{2,1,0:T(8,128)(2,1)S(1)}, u32[]{:S(2)}, u32[]{:S(2)}) async-start(bf16[8,5,4096]{2,1,0:T(8,128)(2,1)} %copy.58), calls=%async_computation.3 | async-start | bytes 1048576 | tf_op jit(solution)/shard_map/while/body/eval_jaxpr/all_to_all | solution.py:107
  370.5 9.3 all-to-all-start.4
  381.4 6.9 collective-permute-start.3
  392.6 6.7 collective-permute-start
  393.8 5.5 collective-permute-start.1
  455.0 20.6 %all-to-all-start.2 = ((bf16[4,8,5,4096]{3,1,2,0:T(8,128)(2,1)}), bf16[4,8,5,4096]{3,1,2,0:T(8,128)(2,1)S(1)}, u32[]{:S(2)}, u32[]{:S(2)}) async-start(bf16[4,8,5,4096]{3,1,2,0:T(8,128)(2,1)} %copy.57), calls=%async_computation.2 | async-start | bytes 2621440 | tf_op jit(solution)/shard_map/while/body/eval_jaxpr/all_to_all | solution.py:45
  476.8 18.6 %all-to-all-start.3 = ((bf16[8,5,4096]{2,1,0:T(8,128)(2,1)}), bf16[8,5,4096]{2,1,0:T(8,128)(2,1)S(1)}, u32[]{:S(2)}, u32[]{:S(2)}) async-start(bf16[8,5,4096]{2,1,0:T(8,128)(2,1)} %copy.58), calls=%async_computation.3 | async-start | bytes 1048576 | tf_op jit(solution)/shard_map/while/body/eval_jaxpr/all_to_all | solution.py:107
  498.1 9.3 all-to-all-start.4
  509.0 6.9 collective-permute-start.3
  520.2 6.7 collective-permute-start
  582.5 20.6 %all-to-all-start.2 = ((bf16[4,8,5,4096]{3,1,2,0:T(8,128)(2,1)}), bf16[4,8,5,4096]{3,1,2,0:T(8,128)(2,1)S(1)}, u32[]{:S(2)}, u32[]{:S(2)}) async-start(bf16[4,8,5,4096]{3,1,2,0:T(8,128)(2,1)} %copy.57), calls=%async_computation.2 | async-start | bytes 2621440 | tf_op jit(solution)/shard_map/while/body/eval_jaxpr/all_to_all | solution.py:45
  604.4 18.6 %all-to-all-start.3 = ((bf16[8,5,4096]{2,1,0:T(8,128)(2,1)}), bf16[8,5,4096]{2,1,0:T(8,128)(2,1)S(1)}, u32[]{:S(2)}, u32[]{:S(2)}) async-start(bf16[8,5,4096]{2,1,0:T(8,128)(2,1)} %copy.58), calls=%async_computation.3 | async-start | bytes 1048576 | tf_op jit(solution)/shard_map/while/body/eval_jaxpr/all_to_all | solution.py:107
  625.6 9.3 all-to-all-start.4
  636.5 6.9 collective-permute-start.3
  647.7 6.7 collective-permute-start
  710.1 20.6 %all-to-all-start.2 = ((bf16[4,8,5,4096]{3,1,2,0:T(8,128)(2,1)}), bf16[4,8,5,4096]{3,1,2,0:T(8,128)(2,1)S(1)}, u32[]{:S(2)}, u32[]{:S(2)}) async-start(bf16[4,8,5,4096]{3,1,2,0:T(8,128)(2,1)} %copy.57), calls=%async_computation.2 | async-start | bytes 2621440 | tf_op jit(solution)/shard_map/while/body/eval_jaxpr/all_to_all | solution.py:45
  731.9 18.6 %all-to-all-start.3 = ((bf16[8,5,4096]{2,1,0:T(8,128)(2,1)}), bf16[8,5,4096]{2,1,0:T(8,128)(2,1)S(1)}, u32[]{:S(2)}, u32[]{:S(2)}) async-start(bf16[8,5,4096]{2,1,0:T(8,128)(2,1)} %copy.58), calls=%async_computation.3 | async-start | bytes 1048576 | tf_op jit(solution)/shard_map/while/body/eval_jaxpr/all_to_all | solution.py:107
  753.2 9.3 all-to-all-start.4
  764.1 6.9 collective-permute-start.3
  775.3 6.7 collective-permute-start
  837.7 20.6 %all-to-all-start.2 = ((bf16[4,8,5,4096]{3,1,2,0:T(8,128)(2,1)}), bf16[4,8,5,4096]{3,1,2,0:T(8,128)(2,1)S(1)}, u32[]{:S(2)}, u32[]{:S(2)}) async-start(bf16[4,8,5,4096]{3,1,2,0:T(8,128)(2,1)} %copy.57), calls=%async_computation.2 | async-start | bytes 2621440 | tf_op jit(solution)/shard_map/while/body/eval_jaxpr/all_to_all | solution.py:45
  859.5 18.6 %all-to-all-start.3 = ((bf16[8,5,4096]{2,1,0:T(8,128)(2,1)}), bf16[8,5,4096]{2,1,0:T(8,128)(2,1)S(1)}, u32[]{:S(2)}, u32[]{:S(2)}) async-start(bf16[8,5,4096]{2,1,0:T(8,128)(2,1)} %copy.58), calls=%async_computation.3 | async-start | bytes 1048576 | tf_op jit(solution)/shard_map/while/body/eval_jaxpr/all_to_all | solution.py:107
  880.8 9.3 all-to-all-start.4
  891.7 6.9 collective-permute-start.3
  902.9 6.7 collective-permute-start
  965.3 20.6 %all-to-all-start.2 = ((bf16[4,8,5,4096]{3,1,2,0:T(8,128)(2,1)}), bf16[4,8,5,4096]{3,1,2,0:T(8,128)(2,1)S(1)}, u32[]{:S(2)}, u32[]{:S(2)}) async-start(bf16[4,8,5,4096]{3,1,2,0:T(8,128)(2,1)} %copy.57), calls=%async_computation.2 | async-start | bytes 2621440 | tf_op jit(solution)/shard_map/while/body/eval_jaxpr/all_to_all | solution.py:45
  987.1 18.6 %all-to-all-start.3 = ((bf16[8,5,4096]{2,1,0:T(8,128)(2,1)}), bf16[8,5,4096]{2,1,0:T(8,128)(2,1)S(1)}, u32[]{:S(2)}, u32[]{:S(2)}) async-start(bf16[8,5,4096]{2,1,0:T(8,128)(2,1)} %copy.58), calls=%async_computation.3 | async-start | bytes 1048576 | tf_op jit(solution)/shard_map/while/body/eval_jaxpr/all_to_all | solution.py:107
  1008.3 9.3 all-to-all-start.4
  1019.2 6.9 collective-permute-start.3
  1030.5 6.7 collective-permute-start
  1031.7 5.5 collective-permute-start.1
  1092.8 20.6 %all-to-all-start.2 = ((bf16[4,8,5,4096]{3,1,2,0:T(8,128)(2,1)}), bf16[4,8,5,4096]{3,1,2,0:T(8,128)(2,1)S(1)}, u32[]{:S(2)}, u32[]{:S(2)}) async-start(bf16[4,8,5,4096]{3,1,2,0:T(8,128)(2,1)} %copy.57), calls=%async_computation.2 | async-start | bytes 2621440 | tf_op jit(solution)/shard_map/while/body/eval_jaxpr/all_to_all | solution.py:45
  1114.7 18.6 %all-to-all-start.3 = ((bf16[8,5,4096]{2,1,0:T(8,128)(2,1)}), bf16[8,5,4096]{2,1,0:T(8,128)(2,1)S(1)}, u32[]{:S(2)}, u32[]{:S(2)}) async-start(bf16[8,5,4096]{2,1,0:T(8,128)(2,1)} %copy.58), calls=%async_computation.3 | async-start | bytes 1048576 | tf_op jit(solution)/shard_map/while/body/eval_jaxpr/all_to_all | solution.py:107
  1135.9 9.3 all-to-all-start.4
  1146.8 6.9 collective-permute-start.3
  (96 other events, 861.8 us)
